TPU v7x, 32 devices: a whole 2x2x4 slice. The times are simulated.
32 devices in a mesh: grp: 2 (over x), aux: 16 (over z, y, core).
Axes of the slice: x: 2, y: 2, z: 4, core: 2. Of those that a mesh axis runs over, the one named last changes fastest.
Arguments:
- three_index: bfloat16 [64, 256, 256], P('aux'), may hold values from -0.375 to 0.375
- relaxed: bfloat16 [512, 256], P('grp'), parts along dimension 0, may hold values from -0.375 to 0.375
- plus_amplitude: bfloat16 [512, 256], P('grp'), parts along dimension 0, may hold values from -0.375 to 0.375
- minus_amplitude: bfloat16 [512, 256], P('grp'), parts along dimension 0, may hold values from -0.375 to 0.375
- ground: bfloat16 [256, 256], replicated, may hold values from -0.375 to 0.375
- integral_grad: bfloat16 [3, 64, 512, 256], P(None, None, 'aux'), may hold values from -0.09375 to 0.09375
- metric_grad: bfloat16 [3, 64, 64], P(None, 'aux'), may hold values from -0.5 to 0.5
- function_atom: int32 [256], replicated, may hold values from 0 to 31, never falling along the last dimension, each value on 1 to 16 neighbouring positions
- aux_center: int32 [64], P('aux'), may hold values from 0 to 31, never falling along the last dimension, each value on 1 to 4 neighbouring positions
- block_list: int32 [512], replicated, may hold values from 0 to 255, as said below
- block_count: int32 [16], replicated, may hold values from 0 to 32, as said below
Outputs:
- gradient: float32 [3, 64], P(None, 'grp'), parts along dimension 1
There are 2 independent parts, one for each index of `grp`. A program takes and returns all parts, laid end to end along the dimension named above; an argument that names none is the same for every part. Nothing has to cross between parts.
Inputs may be any that keep to these rules, and one draw needn't show every extreme that they name: block_count[d] is the number of live slots of owner d; the counts sum to 256, and at least one owner has 32. `block_list`: slot s of owner d is entry d * 32 + s and is live when s < block_count[d]; each tile pair i * 16 + j is held by exactly one live slot; slots that are not live hold arbitrary tile pairs.
All inputs are finite; a program needn't handle non-finite values.
Results may differ from a plain program's by a relative error of at most 0.0032.
Values may be sent and summed in bfloat16 or wider, within the bound.
No kernel may reach another device: no remote copies, remote signals or barrier semaphores. Data moves between devices by JAX's collectives and lax.ppermute only.
A program may use at most 64 MiB of HBM per device.

v0:
```python
import jax
import jax.numpy as jnp
from jax import lax
from jax.sharding import PartitionSpec as P

TILE = 16
NATOM = 32


def on_device(
    three_index,
    relaxed,
    plus_amplitude,
    minus_amplitude,
    ground,
    integral_grad,
    metric_grad,
    function_atom,
    aux_center,
    block_list,
    block_count,
):
    highest = lax.Precision.HIGHEST
    aux_local = three_index.shape[0]
    basis_count = three_index.shape[1]
    tile_count = basis_count // TILE
    slot_depth = integral_grad.shape[2]
    slot_total = block_list.shape[0]
    fitted = jnp.einsum("pab,ab->p", three_index, relaxed, preferred_element_type=jnp.float32)
    stacked = jnp.concatenate([plus_amplitude, minus_amplitude, ground], 0)
    halves = jnp.einsum(
        "ab,pbc->pac", stacked, three_index, preferred_element_type=jnp.float32
    ).astype(jnp.bfloat16)
    paired_half = halves[:, : 2 * basis_count].reshape(aux_local, 2, basis_count, basis_count)
    paired_half = jnp.concatenate([paired_half[:, 0], paired_half[:, 1]], axis=2)
    ground_half = halves[:, 2 * basis_count :]
    partners = jnp.concatenate([plus_amplitude, -minus_amplitude], axis=1)
    exchange_part = jnp.einsum(
        "pab,cb->pac", paired_half, partners, preferred_element_type=jnp.float32
    )
    crossed = jnp.einsum("pab,bc->pac", ground_half, relaxed, preferred_element_type=jnp.float32)
    triple = (
        fitted[:, None, None] * relaxed.astype(jnp.float32)[None]
        + exchange_part
        + crossed
        + jnp.swapaxes(crossed, 1, 2)
    )
    triple = triple.astype(jnp.bfloat16)
    blocked = triple.reshape(aux_local, tile_count, TILE, tile_count, TILE).transpose(0, 1, 3, 2, 4)
    blocked = blocked.reshape(aux_local, tile_count * tile_count, TILE * TILE)
    chosen = jnp.take(blocked, block_list, axis=1)
    slot_ids = jnp.arange(slot_total, dtype=jnp.int32)
    live_mask = (slot_ids % slot_depth < block_count[slot_ids // slot_depth]).astype(jnp.float32)
    arrived = lax.all_to_all(chosen, "aux", split_axis=1, concat_axis=0, tiled=True)
    first_slot = lax.axis_index("aux") * slot_depth
    tile_ids = lax.dynamic_slice_in_dim(block_list, first_slot, slot_depth)
    slot_mask = lax.dynamic_slice_in_dim(live_mask, first_slot, slot_depth)
    contracted = jnp.einsum(
        "pgf,kpgf->kgf", arrived, integral_grad, preferred_element_type=jnp.float32
    )
    slot_count = tile_ids.shape[0]
    row_sums = contracted.reshape(3, slot_count, TILE, TILE).sum(axis=3) * slot_mask[None, :, None]
    function_ids = (tile_ids // tile_count)[:, None] * TILE + jnp.arange(TILE, dtype=jnp.int32)[
        None, :
    ]
    atom_table = (
        function_atom[function_ids][:, :, None] == jnp.arange(NATOM, dtype=jnp.int32)[None, None, :]
    ).astype(jnp.float32)
    three_part = 2.0 * jnp.einsum("kgm,gma->ka", row_sums, atom_table, precision=highest)
    all_fitted = lax.all_gather(fitted, "aux", axis=0, tiled=True)
    coupling = jnp.einsum(
        "kpq,q->kp", metric_grad.astype(jnp.float32), all_fitted, precision=highest
    )
    aux_table = (aux_center[:, None] == jnp.arange(NATOM, dtype=jnp.int32)[None, :]).astype(
        jnp.float32
    )
    metric_part = jnp.einsum("kp,pa->ka", coupling * fitted[None, :], aux_table, precision=highest)
    return lax.psum(three_part - metric_part, "aux")


def solution(mesh):
    in_specs = (
        P("aux", None, None),
        P("grp", None),
        P("grp", None),
        P("grp", None),
        P(),
        P(None, None, "aux", None),
        P(None, "aux", None),
        P(),
        P("aux"),
        P(),
        P(),
    )
    out_specs = P(None, "grp")
    return jax.shard_map(
        on_device, mesh=mesh, in_specs=in_specs, out_specs=out_specs, check_vma=False
    )
```

profile of v0, /device:TPU:0, one launch (start us, length us, event | category | flops | bytes accessed | tf_op | source)
XLA Modules:
  0.0 119.7 jit_solution(17670021363365028496)
XLA Ops:
  0.0 1.8 %fusion = bf16[4,768,256]{2,1,0:T(8,128)(2,1)S(1)} fusion(bf16[4,256,256]{2,1,0:T(8,128)(2,1)} %param.11, bf16[256,256]{1,0:T(8,128)(2,1)} %param.15, bf16[256,256]{1,0:T(8,128)(2,1)} %param.14, bf16[256,256]{1,0:T(8,128)(2,1)} %param.13), kind=kOutput, calls=%fused_computation.5 | convolution fusion | flops 404619264 | bytes 2490368 | tf_op jit(solution)/shard_map/ab,pbc->pac/dot_general | solution.py:31
  2.3 0.5 copy-done.6
  2.8 0.7 neg.3
  3.5 0.9 slice_bitcast_fusion.1
  4.3 0.3 copy.42
  4.7 1.9 %convolution_bitcast_fusion.1 = f32[4]{0:T(128)S(1)} fusion(bf16[4,256,256]{2,1,0:T(8,128)(2,1)S(1)} %copy-done.4, bf16[256,256,1]{1,0,2:T(8,128)(2,1)} %bitcast.80), kind=kOutput, calls=%fused_computation.13 | convolution fusion | flops 524288 | bytes 655376 | tf_op jit(solution)/shard_map/pab,ab->p/dot_general | solution.py:29
  6.6 0.5 copy-done.11
  7.1 0.5 fusion.3
  7.6 4.2 %reshape.108 = bf16[4,16,16,16,16]{4,3,2,1,0:T(8,128)(2,1)} reshape(bf16[4,256,256]{2,1,0:T(8,128)(2,1)S(1)} %fusion.3) | data formatting | bytes 1048576 | tf_op jit(solution)/shard_map/reshape | solution.py:49
  11.7 5.2 %copy.74 = bf16[4,16,16,16,16]{4,2,3,1,0:T(8,128)(2,1)} copy(bf16[4,16,16,16,16]{4,3,2,1,0:T(8,128)(2,1)} %reshape.108) | data formatting | bytes 1048576 | tf_op jit(solution)/shard_map/reshape | solution.py:49
  17.0 5.5 %reshape.109 = bf16[4,256,256]{2,1,0:T(8,128)(2,1)S(1)} reshape(bf16[4,16,16,16,16]{4,3,2,1,0:T(8,128)(2,1)} %bitcast.77) | data formatting | bytes 1048576 | tf_op jit(solution)/shard_map/reshape | solution.py:50
  22.5 0.4 copy.44
  22.9 2.4 %gather_fusion = bf16[512,4,256]{2,1,0:T(4,128)(2,1)S(1)} fusion(bf16[4,256,256]{2,0,1:T(4,128)(2,1)S(1)} %copy.44, s32[1024]{0:T(1024)S(1)} %pad_clamp_fusion.1), kind=kCustom, calls=%fused_computation | custom fusion | bytes 2099200 | tf_op jit(solution)/shard_map/jit(_take)/gather | solution.py:51
  25.3 2.7 %select_bitcast_fusion = bf16[4,512,256]{2,0,1:T(4,128)(2,1)} fusion(bf16[512,4,256]{2,1,0:T(4,128)(2,1)S(1)} %gather_fusion, pred[512]{0:T(512)(128)(4,1)S(1)} %compare_and_fusion), kind=kLoop, calls=%fused_computation.18 | loop fusion | flops 524288 | bytes 2097664 | tf_op jit(solution)/shard_map/jit(_take)/select_n | solution.py:51
  28.0 7.4 %all-to-all-start = ((bf16[4,512,256]{2,0,1:T(4,128)(2,1)}), bf16[4,512,256]{2,0,1:T(4,128)(2,1)S(1)}, u32[]{:S(2)}, u32[]{:S(2)}) async-start(bf16[4,512,256]{2,0,1:T(4,128)(2,1)} %select_bitcast_fusion), calls=%async_computation | async-start | bytes 2097152 | tf_op jit(solution)/shard_map/all_to_all | solution.py:54
  35.7 0.7 fusion.34
  36.5 4.3 %compare_select_fusion.2 = s32[512,1]{0,1:T(1,128)S(1)} fusion(s32[]{:T(128)} %bitcast.30, s32[]{:T(128)} %bitcast.31, s32[]{:T(128)} %bitcast.32, s32[]{:T(128)} %bitcast.33, s32[]{:T(128)} %bitcast.34, s32[]{:T(128)} %bitcast.36, s32[]{:T(128)} %bitcast.35), kind=kLoop, calls=%fused_computation.49 | loop fusion | flops 11776 | bytes 2076 | tf_op jit(solution)/shard_map/gather | solution.py:53
  40.8 5.7 %fusion.25 = f32[512]{0:T(512)S(1)} fusion(pred[512]{0:T(512)(128)(4,1)S(1)} %compare_reduce_fusion, pred[512]{0:T(512)(128)(4,1)S(1)} %compare_reduce_fusion.1, pred[512]{0:T(512)(128)(4,1)S(1)} %compare_reduce_fusion.2, pred[512]{0:T(512)(128)(4,1)S(1)} %compare_reduce_fusion.3, pred[512]{0:T(512)(128)(4,1)S(1)} %compare_reduce_fusion.4, ...), kind=kLoop, calls=%fused_computation.73 | loop fusion | flops 8704 | bytes 8740 | tf_op jit(solution)/shard_map/convert_element_type | solution.py:53
  46.8 3.5 %gather_fusion.1 = s32[512]{0:T(512)S(1)} fusion(s32[256]{0:T(256)S(1)} %copy-done.1, s32[1024]{0:T(1024)S(1)} %pad_clamp_fusion), kind=kCustom, calls=%fused_computation.1 | custom fusion | bytes 6144 | tf_op jit(solution)/shard_map/gather | solution.py:67
  50.5 0.6 dynamic-slice
  52.0 33.9 %all-reduce = f32[64]{0:T(128)S(1)} all-reduce(f32[64]{0:T(128)S(1)} %dynamic-update-slice), channel_id=1, replica_groups=mesh['grp'=2,'aux'=16] {'aux'}, use_global_device_ids=true, to_apply=%add | all-reduce | flops 64 | bytes 512
  86.6 1.5 %copy-done.2 = bf16[3,64,32,256]{3,2,1,0:T(8,128)(2,1)S(1)} copy-done((bf16[3,64,32,256]{3,2,1,0:T(8,128)(2,1)S(1)}, bf16[3,64,32,256]{3,2,1,0:T(8,128)(2,1)}, u32[]{:S(2)}) %copy-start.2) | copy-done | bytes 3145752
  88.2 0.7 multiply_reduce_fusion
  89.7 30.1 %psum.7 = f32[3,32]{1,0:T(4,128)} all-reduce(f32[3,32]{1,0:T(4,128)S(1)} %convolution_subtract_fusion), channel_id=1, replica_groups=mesh['grp'=2,'aux'=16] {'aux'}, use_global_device_ids=true, to_apply=%region_1.2 | all-reduce | flops 96 | bytes 768 | tf_op jit(solution)/shard_map/psum | solution.py:78
  (60 shorter events, 2.9 us)
Async XLA Ops:
  0.0 85.9 %copy-start = (bf16[3,4,64]{2,1,0:T(4,128)(2,1)S(1)}, bf16[3,4,64]{2,1,0:T(4,128)(2,1)}, u32[]{:S(2)}) copy-start(bf16[3,4,64]{2,1,0:T(4,128)(2,1)} %param.17) | copy-start | bytes 4612
  0.0 2.0 %copy-start.8 = (bf16[256,256]{1,0:T(8,128)(2,1)S(1)}, bf16[256,256]{1,0:T(8,128)(2,1)}, u32[]{:S(2)}) copy-start(bf16[256,256]{1,0:T(8,128)(2,1)} %param.12) | copy-start | bytes 393220
  1.9 0.9 copy-start.6
  1.9 1.6 %copy-start.10 = (s32[512]{0:T(512)S(1)}, s32[512]{0:T(512)}, u32[]{:S(2)}) copy-start(s32[512]{0:T(512)} %param.20) | copy-start | bytes 6148
  3.5 1.2 %copy-start.4 = (bf16[4,256,256]{2,1,0:T(8,128)(2,1)S(1)}, bf16[4,256,256]{2,1,0:T(8,128)(2,1)}, u32[]{:S(2)}) copy-start(bf16[4,256,256]{2,1,0:T(8,128)(2,1)} %param.11) | copy-start | bytes 1572868
  4.3 2.8 %copy-start.5 = (bf16[256,256]{1,0:T(8,128)(2,1)S(1)}, bf16[256,256]{1,0:T(8,128)(2,1)}, u32[]{:S(2)}) copy-start(bf16[256,256]{1,0:T(8,128)(2,1)} %param.13) | copy-start | bytes 393220
  4.7 2.4 %copy-start.3 = (bf16[4,256,256]{2,1,0:T(8,128)(2,1)S(1)}, bf16[4,256,256]{2,1,0:T(8,128)(2,1)}, u32[]{:S(2)}) copy-start(bf16[4,256,256]{2,1,0:T(8,128)(2,1)} %get-tuple-element.6) | copy-start | bytes 1572868
  4.7 2.4 %copy-start.7 = (bf16[256,256]{1,0:T(8,128)(2,1)S(1)}, bf16[256,256]{1,0:T(8,128)(2,1)}, u32[]{:S(2)}) copy-start(bf16[256,256]{1,0:T(8,128)(2,1)} %neg.3) | copy-start | bytes 393220
  6.6 0.5 copy-start.11
  25.3 10.4 %copy-start.9 = (s32[16]{0:T(128)S(1)}, s32[16]{0:T(128)}, u32[]{:S(2)}) copy-start(s32[16]{0:T(128)} %param.21) | copy-start | bytes 196
  25.3 21.4 %copy-start.1 = (s32[256]{0:T(256)S(1)}, s32[256]{0:T(256)}, u32[]{:S(2)}) copy-start(s32[256]{0:T(256)} %param.18) | copy-start | bytes 3076
  28.0 58.0 %all-to-all-start = ((bf16[4,512,256]{2,0,1:T(4,128)(2,1)}), bf16[4,512,256]{2,0,1:T(4,128)(2,1)S(1)}, u32[]{:S(2)}, u32[]{:S(2)}) async-start(bf16[4,512,256]{2,0,1:T(4,128)(2,1)} %select_bitcast_fusion), calls=%async_computation | async-start | bytes 2097152 | tf_op jit(solution)/shard_map/all_to_all | solution.py:54
  46.8 3.7 %copy-start.14 = (u32[32]{0:T(128)S(1)}, u32[32]{0:T(128)}, u32[]{:S(2)}) copy-start(u32[32]{0:T(128)} %constant.97) | copy-start | bytes 388
  46.8 4.9 %copy-start.12 = (f32[4]{0:T(128)S(1)}, f32[4]{0:T(128)}, u32[]{:S(2)}) copy-start(f32[4]{0:T(128)} %copy-done.11) | copy-start | bytes 52
  86.3 1.9 %copy-start.2 = (bf16[3,64,32,256]{3,2,1,0:T(8,128)(2,1)S(1)}, bf16[3,64,32,256]{3,2,1,0:T(8,128)(2,1)}, u32[]{:S(2)}) copy-start(bf16[3,64,32,256]{3,2,1,0:T(8,128)(2,1)} %param.16) | copy-start | bytes 9437188
  88.2 1.3 %copy-start.13 = (s32[4]{0:T(128)S(1)}, s32[4]{0:T(128)}, u32[]{:S(2)}) copy-start(s32[4]{0:T(128)} %param.19) | copy-start | bytes 52
where the time goes:
time: 120 us
  blocking collectives  64 us (53%)
  local copies, waits for them, and re-layouts  27.3 us (23%)
  other arithmetic  15 us (12%)
  starting transfers between devices  7.41 us (6%)
  matrix products  5.13 us (4%)
    unnamed x1, blocking collectives  33.9 us
    psum x1, blocking collectives, on_device(): return lax.psum(three_part - metric_part, 'aux')  30.1 us
    reshape x2, local copies, waits for them, and re-layouts, on_device(): triple.reshape(aux_local, tile_count, TILE, tile_count, TILE)  9.39 us
    all_to_all x1, starting transfers between devices, on_device(): lax.all_to_all(chosen, 'aux', split_axis=1, concat_axis=0, tiled=True)  7.41 us
    reshape x2, local copies, waits for them, and re-layouts, on_device(): blocked = blocked.reshape(aux_local, tile_count * tile_count, TILE * TILE)  5.89 us
    convert_element_type x1, other arithmetic, on_device(): (slot_ids % slot_depth < block_count[slot_ids // slot_depth]).astype(jnp....  5.67 us
    gather x10, other arithmetic, on_device(): block_count[slot_ids // slot_depth]  4.61 us
    gather x3, local copies, waits for them, and re-layouts, on_device(): function_atom[function_ids][:, :, None]  3.67 us
  transfers between devices with their start and end apart: 1, of which 0 were waited for; matrix products, arithmetic and copies ran while one was open for 13% of the time, Pallas kernels for 0%

commit v1 on v0

--- a/solution.py
+++ b/solution.py
@@ -5,6 +5,12 @@
 
 TILE = 16
 NATOM = 32
+
+
+def gather_and_add(array, name):
+    shards = lax.all_gather(array, name, axis=0, tiled=False)
+    summed = shards.sum(axis=0)
+    return summed
 
 
 def on_device(
@@ -75,7 +81,7 @@
         jnp.float32
     )
     metric_part = jnp.einsum("kp,pa->ka", coupling * fitted[None, :], aux_table, precision=highest)
-    return lax.psum(three_part - metric_part, "aux")
+    return gather_and_add(three_part - metric_part, "aux")
 
 
 def solution(mesh):

time: 120 us -> 108 us (0.900)
  blocking collectives: 64 us -> 51.1 us
    psum x1 -> x0, blocking collectives: 30.1 us -> none  [on_device(): return lax.psum(three_part - metric_part, 'aux')]
    all_gather x0 -> x1, blocking collectives: none -> 17.2 us  [gather_and_add(): shards = lax.all_gather(array, name, axis=0, tiled=False)]
  transfers between devices with their start and end apart: 1 -> 1, of which waited for: 0 -> 0; matrix products, arithmetic and copies ran while one was open for 13% -> 15% of each run, Pallas kernels for 0% -> 0%
where the time goes in v1:
time: 108 us; the launch traced here: 107 us
  blocking collectives  51.1 us (47%)
  local copies, waits for them, and re-layouts  27.3 us (25%)
  other arithmetic  15.6 us (14%)
  starting transfers between devices  7.41 us (7%)
  matrix products  5.13 us (5%)
    unnamed x1, blocking collectives  33.9 us
    all_gather x1, blocking collectives, gather_and_add(): shards = lax.all_gather(array, name, axis=0, tiled=False)  17.2 us
    reshape x2, local copies, waits for them, and re-layouts, on_device(): triple.reshape(aux_local, tile_count, TILE, tile_count, TILE)  9.39 us
    all_to_all x1, starting transfers between devices, on_device(): lax.all_to_all(chosen, 'aux', split_axis=1, concat_axis=0, tiled=True)  7.41 us
    reshape x2, local copies, waits for them, and re-layouts, on_device(): blocked = blocked.reshape(aux_local, tile_count * tile_count, TILE * TILE)  5.89 us
    convert_element_type x1, other arithmetic, on_device(): (slot_ids % slot_depth < block_count[slot_ids // slot_depth]).astype(jnp....  5.67 us
    gather x10, other arithmetic, on_device(): block_count[slot_ids // slot_depth]  4.61 us
    gather x3, local copies, waits for them, and re-layouts, on_device(): function_atom[function_ids][:, :, None]  3.67 us
  transfers between devices with their start and end apart: 1, of which 0 were waited for; matrix products, arithmetic and copies ran while one was open for 15% of the time, Pallas kernels for 0%

profile of v1, /device:TPU:0, one launch (start us, length us, event | category | flops | bytes accessed | tf_op | source)
XLA Modules:
  0.0 107.5 jit_solution(15786463537390900283)
XLA Ops:
  0.0 1.8 %fusion = bf16[4,768,256]{2,1,0:T(8,128)(2,1)S(1)} fusion(bf16[4,256,256]{2,1,0:T(8,128)(2,1)} %param.11, bf16[256,256]{1,0:T(8,128)(2,1)} %param.15, bf16[256,256]{1,0:T(8,128)(2,1)} %param.14, bf16[256,256]{1,0:T(8,128)(2,1)} %param.13), kind=kOutput, calls=%fused_computation.5 | convolution fusion | flops 404619264 | bytes 2490368 | tf_op jit(solution)/shard_map/ab,pbc->pac/dot_general | solution.py:37
  2.3 0.5 copy-done.6
  2.8 0.7 neg.3
  3.5 0.9 slice_bitcast_fusion.1
  4.7 1.9 %convolution_bitcast_fusion.1 = f32[4]{0:T(128)S(1)} fusion(bf16[4,256,256]{2,1,0:T(8,128)(2,1)S(1)} %copy-done.4, bf16[256,256,1]{1,0,2:T(8,128)(2,1)} %bitcast.82), kind=kOutput, calls=%fused_computation.14 | convolution fusion | flops 524288 | bytes 655376 | tf_op jit(solution)/shard_map/pab,ab->p/dot_general | solution.py:35
  6.6 0.5 copy-done.11
  7.1 0.5 fusion.3
  7.6 4.2 %reshape.108 = bf16[4,16,16,16,16]{4,3,2,1,0:T(8,128)(2,1)} reshape(bf16[4,256,256]{2,1,0:T(8,128)(2,1)S(1)} %fusion.3) | data formatting | bytes 1048576 | tf_op jit(solution)/shard_map/reshape | solution.py:55
  11.7 5.2 %copy.81 = bf16[4,16,16,16,16]{4,2,3,1,0:T(8,128)(2,1)} copy(bf16[4,16,16,16,16]{4,3,2,1,0:T(8,128)(2,1)} %reshape.108) | data formatting | bytes 1048576 | tf_op jit(solution)/shard_map/reshape | solution.py:55
  17.0 5.5 %reshape.109 = bf16[4,256,256]{2,1,0:T(8,128)(2,1)S(1)} reshape(bf16[4,16,16,16,16]{4,3,2,1,0:T(8,128)(2,1)} %bitcast.79) | data formatting | bytes 1048576 | tf_op jit(solution)/shard_map/reshape | solution.py:56
  22.5 0.4 copy.51
  22.9 2.4 %gather_fusion = bf16[512,4,256]{2,1,0:T(4,128)(2,1)S(1)} fusion(bf16[4,256,256]{2,0,1:T(4,128)(2,1)S(1)} %copy.51, s32[1024]{0:T(1024)S(1)} %pad_clamp_fusion.1), kind=kCustom, calls=%fused_computation | custom fusion | bytes 2099200 | tf_op jit(solution)/shard_map/jit(_take)/gather | solution.py:57
  25.3 2.7 %select_bitcast_fusion = bf16[4,512,256]{2,0,1:T(4,128)(2,1)} fusion(bf16[512,4,256]{2,1,0:T(4,128)(2,1)S(1)} %gather_fusion, pred[512]{0:T(512)(128)(4,1)S(1)} %compare_and_fusion), kind=kLoop, calls=%fused_computation.19 | loop fusion | flops 524288 | bytes 2097664 | tf_op jit(solution)/shard_map/jit(_take)/select_n | solution.py:57
  28.0 7.4 %all-to-all-start = ((bf16[4,512,256]{2,0,1:T(4,128)(2,1)}), bf16[4,512,256]{2,0,1:T(4,128)(2,1)S(1)}, u32[]{:S(2)}, u32[]{:S(2)}) async-start(bf16[4,512,256]{2,0,1:T(4,128)(2,1)} %select_bitcast_fusion), calls=%async_computation | async-start | bytes 2097152 | tf_op jit(solution)/shard_map/all_to_all | solution.py:60
  35.7 0.7 fusion.35
  36.5 4.3 %compare_select_fusion.2 = s32[512,1]{0,1:T(1,128)S(1)} fusion(s32[]{:T(128)} %bitcast.30, s32[]{:T(128)} %bitcast.31, s32[]{:T(128)} %bitcast.32, s32[]{:T(128)} %bitcast.33, s32[]{:T(128)} %bitcast.34, s32[]{:T(128)} %bitcast.36, s32[]{:T(128)} %bitcast.35), kind=kLoop, calls=%fused_computation.50 | loop fusion | flops 11776 | bytes 2076 | tf_op jit(solution)/shard_map/gather | solution.py:59
  40.8 5.7 %fusion.26 = f32[512]{0:T(512)S(1)} fusion(pred[512]{0:T(512)(128)(4,1)S(1)} %compare_reduce_fusion, pred[512]{0:T(512)(128)(4,1)S(1)} %compare_reduce_fusion.1, pred[512]{0:T(512)(128)(4,1)S(1)} %compare_reduce_fusion.2, pred[512]{0:T(512)(128)(4,1)S(1)} %compare_reduce_fusion.3, pred[512]{0:T(512)(128)(4,1)S(1)} %compare_reduce_fusion.4, ...), kind=kLoop, calls=%fused_computation.74 | loop fusion | flops 8704 | bytes 8740 | tf_op jit(solution)/shard_map/convert_element_type | solution.py:59
  46.8 3.5 %gather_fusion.1 = s32[512]{0:T(512)S(1)} fusion(s32[256]{0:T(256)S(1)} %copy-done.1, s32[1024]{0:T(1024)S(1)} %pad_clamp_fusion), kind=kCustom, calls=%fused_computation.1 | custom fusion | bytes 6144 | tf_op jit(solution)/shard_map/gather | solution.py:73
  50.5 0.6 dynamic-slice
  52.0 33.9 %all-reduce = f32[64]{0:T(128)S(1)} all-reduce(f32[64]{0:T(128)S(1)} %dynamic-update-slice), channel_id=1, replica_groups=mesh['grp'=2,'aux'=16] {'aux'}, use_global_device_ids=true, to_apply=%add | all-reduce | flops 64 | bytes 512
  86.6 1.5 %copy-done.2 = bf16[3,64,32,256]{3,2,1,0:T(8,128)(2,1)S(1)} copy-done((bf16[3,64,32,256]{3,2,1,0:T(8,128)(2,1)S(1)}, bf16[3,64,32,256]{3,2,1,0:T(8,128)(2,1)}, u32[]{:S(2)}) %copy-start.2) | copy-done | bytes 3145752
  88.2 0.7 multiply_reduce_fusion
  89.7 17.2 %all-gather.1 = f32[16,3,32]{2,1,0:T(4,128)S(1)} all-gather(f32[1,3,32]{2,1,0:T(4,128)S(1)} %fusion.4), channel_id=2, replica_groups=mesh['grp'=2,'aux'=16] {'aux'}, dimensions={0}, use_global_device_ids=true | all-gather | bytes 6528 | tf_op jit(solution)/shard_map/all_gather | solution.py:11
  106.9 0.6 reduce_sum.19
  (61 shorter events, 3.2 us)
Async XLA Ops:
  0.0 85.9 %copy-start = (bf16[3,4,64]{2,1,0:T(4,128)(2,1)S(1)}, bf16[3,4,64]{2,1,0:T(4,128)(2,1)}, u32[]{:S(2)}) copy-start(bf16[3,4,64]{2,1,0:T(4,128)(2,1)} %param.17) | copy-start | bytes 4612
  0.0 2.0 %copy-start.8 = (bf16[256,256]{1,0:T(8,128)(2,1)S(1)}, bf16[256,256]{1,0:T(8,128)(2,1)}, u32[]{:S(2)}) copy-start(bf16[256,256]{1,0:T(8,128)(2,1)} %param.12) | copy-start | bytes 393220
  1.9 0.9 copy-start.6
  1.9 1.6 %copy-start.10 = (s32[512]{0:T(512)S(1)}, s32[512]{0:T(512)}, u32[]{:S(2)}) copy-start(s32[512]{0:T(512)} %param.20) | copy-start | bytes 6148
  3.5 1.2 %copy-start.4 = (bf16[4,256,256]{2,1,0:T(8,128)(2,1)S(1)}, bf16[4,256,256]{2,1,0:T(8,128)(2,1)}, u32[]{:S(2)}) copy-start(bf16[4,256,256]{2,1,0:T(8,128)(2,1)} %param.11) | copy-start | bytes 1572868
  4.3 2.8 %copy-start.5 = (bf16[256,256]{1,0:T(8,128)(2,1)S(1)}, bf16[256,256]{1,0:T(8,128)(2,1)}, u32[]{:S(2)}) copy-start(bf16[256,256]{1,0:T(8,128)(2,1)} %param.13) | copy-start | bytes 393220
  4.7 2.4 %copy-start.3 = (bf16[4,256,256]{2,1,0:T(8,128)(2,1)S(1)}, bf16[4,256,256]{2,1,0:T(8,128)(2,1)}, u32[]{:S(2)}) copy-start(bf16[4,256,256]{2,1,0:T(8,128)(2,1)} %get-tuple-element.6) | copy-start | bytes 1572868
  4.7 2.4 %copy-start.7 = (bf16[256,256]{1,0:T(8,128)(2,1)S(1)}, bf16[256,256]{1,0:T(8,128)(2,1)}, u32[]{:S(2)}) copy-start(bf16[256,256]{1,0:T(8,128)(2,1)} %neg.3) | copy-start | bytes 393220
  6.6 0.5 copy-start.11
  25.3 10.4 %copy-start.9 = (s32[16]{0:T(128)S(1)}, s32[16]{0:T(128)}, u32[]{:S(2)}) copy-start(s32[16]{0:T(128)} %param.21) | copy-start | bytes 196
  25.3 21.4 %copy-start.1 = (s32[256]{0:T(256)S(1)}, s32[256]{0:T(256)}, u32[]{:S(2)}) copy-start(s32[256]{0:T(256)} %param.18) | copy-start | bytes 3076
  28.0 58.0 %all-to-all-start = ((bf16[4,512,256]{2,0,1:T(4,128)(2,1)}), bf16[4,512,256]{2,0,1:T(4,128)(2,1)S(1)}, u32[]{:S(2)}, u32[]{:S(2)}) async-start(bf16[4,512,256]{2,0,1:T(4,128)(2,1)} %select_bitcast_fusion), calls=%async_computation | async-start | bytes 2097152 | tf_op jit(solution)/shard_map/all_to_all | solution.py:60
  46.8 3.7 %copy-start.14 = (u32[32]{0:T(128)S(1)}, u32[32]{0:T(128)}, u32[]{:S(2)}) copy-start(u32[32]{0:T(128)} %constant.97) | copy-start | bytes 388
  46.8 4.9 %copy-start.12 = (f32[4]{0:T(128)S(1)}, f32[4]{0:T(128)}, u32[]{:S(2)}) copy-start(f32[4]{0:T(128)} %copy-done.11) | copy-start | bytes 52
  86.3 1.9 %copy-start.2 = (bf16[3,64,32,256]{3,2,1,0:T(8,128)(2,1)S(1)}, bf16[3,64,32,256]{3,2,1,0:T(8,128)(2,1)}, u32[]{:S(2)}) copy-start(bf16[3,64,32,256]{3,2,1,0:T(8,128)(2,1)} %param.16) | copy-start | bytes 9437188
  88.2 1.3 %copy-start.13 = (s32[4]{0:T(128)S(1)}, s32[4]{0:T(128)}, u32[]{:S(2)}) copy-start(s32[4]{0:T(128)} %param.19) | copy-start | bytes 52
